TPU v7x, 32 devices: a whole 2x2x4 slice. The times are simulated.
32 devices in a mesh: fsdp: 2 (over x), ctx: 4 (over z), tp: 4 (over y, core).
Axes of the slice: x: 2, y: 2, z: 4, core: 2. Of those that a mesh axis runs over, the one named last changes fastest.
Arguments:
- tokens: bfloat16 [4, 2048, 1024], P('fsdp', 'ctx'), may hold values from -6 to 6
- segment_ids: int32 [4, 2048], P('fsdp'), may hold values from 0 to 15, never falling along the last dimension, each value on 1 to 1024 neighbouring positions
- attn_gain: bfloat16 [1024], P('fsdp'), may hold values from 0.25 to 1.75
- w_query: bfloat16 [1024, 2048], P('fsdp', 'tp'), may hold values from -0.1875 to 0.1875
- w_key: bfloat16 [1024, 1024], P('fsdp', 'tp'), may hold values from -0.1875 to 0.1875
- w_value: bfloat16 [1024, 1024], P('fsdp', 'tp'), may hold values from -0.1875 to 0.1875
- query_gain: bfloat16 [128], P('fsdp'), may hold values from 0.099609375 to 1.8984375
- key_gain: bfloat16 [128], P('fsdp'), may hold values from 0.099609375 to 1.8984375
- w_out: bfloat16 [2048, 1024], P('tp', 'fsdp'), may hold values from -0.375 to 0.375
- ffn_gain: bfloat16 [1024], P('fsdp'), may hold values from 0.25 to 1.75
- w_gate: bfloat16 [1024, 3072], P('fsdp', 'tp'), may hold values from -0.1875 to 0.1875
- w_up: bfloat16 [1024, 3072], P('fsdp', 'tp'), may hold values from -0.1875 to 0.1875
- w_down: bfloat16 [3072, 1024], P('tp', 'fsdp'), may hold values from -0.21875 to 0.21875
- out_grad: bfloat16 [4, 2048, 1024], P('fsdp', 'ctx'), may hold values from -6 to 6
Outputs:
- layer_out: bfloat16 [4, 2048, 1024], P('fsdp', 'ctx')
- input_grad: float32 [4, 2048, 1024], P('fsdp', 'ctx')
- attn_gain_grad: float32 [1024], P('fsdp')
- w_query_grad: float32 [1024, 2048], P('fsdp', 'tp')
- w_key_grad: float32 [1024, 1024], P('fsdp', 'tp')
- w_value_grad: float32 [1024, 1024], P('fsdp', 'tp')
- query_gain_grad: float32 [128], P('fsdp')
- key_gain_grad: float32 [128], P('fsdp')
- w_out_grad: float32 [2048, 1024], P('tp', 'fsdp')
- ffn_gain_grad: float32 [1024], P('fsdp')
- w_gate_grad: float32 [1024, 3072], P('fsdp', 'tp')
- w_up_grad: float32 [1024, 3072], P('fsdp', 'tp')
- w_down_grad: float32 [3072, 1024], P('tp', 'fsdp')
Inputs may be any that keep to these rules, and one draw needn't show every extreme that they name: `segment_ids`: ids never fall along a sequence, every id of 0 to 15 occurs in each sequence (so the padding segment 0 comes first), a segment has 1 to 1024 positions and some segment exactly 1024.
All inputs are finite; a program needn't handle non-finite values.
Results may differ from a plain program's by a relative error of at most 0.025.
Values may be sent and summed in bfloat16 or wider, within the bound.
No kernel may reach another device: no remote copies, remote signals or barrier semaphores. Data moves between devices by JAX's collectives and lax.ppermute only.
A program may use at most 192 MiB of HBM per device.

v0:
```python
import jax
import jax.numpy as jnp
from jax import lax
from jax.sharding import PartitionSpec as P

epsilon = 1e-06
rope_base = 1000000.0
masked_score = -1e30


def rotate(values, cosine, sine):
    half_size = values.shape[-1] // 2
    first = values[..., :half_size]
    second = values[..., half_size:]
    return jnp.concatenate([first * cosine - second * sine, second * cosine + first * sine], -1)


def inv_scale(values):
    return lax.rsqrt(jnp.mean(values * values, -1, keepdims=True) + epsilon)


def norm_back(values, scale, gain, grad):
    scaled = grad * gain
    return scale * scaled - values * scale * scale * scale * jnp.mean(
        scaled * values, -1, keepdims=True
    )


def body(
    tokens,
    segment_ids,
    attn_gain,
    w_query,
    w_key,
    w_value,
    query_gain,
    key_gain,
    w_out,
    ffn_gain,
    w_gate,
    w_up,
    w_down,
    out_grad,
):
    (
        full_attn_gain,
        full_query,
        full_key,
        full_value,
        full_qgain,
        full_kgain,
        full_out,
        full_ffn_gain,
        full_gate,
        full_up,
        full_down,
    ) = (
        lax.all_gather(attn_gain, "fsdp", axis=0, tiled=True),
        lax.all_gather(w_query, "fsdp", axis=0, tiled=True),
        lax.all_gather(w_key, "fsdp", axis=0, tiled=True),
        lax.all_gather(w_value, "fsdp", axis=0, tiled=True),
        lax.all_gather(query_gain, "fsdp", axis=0, tiled=True),
        lax.all_gather(key_gain, "fsdp", axis=0, tiled=True),
        lax.all_gather(w_out, "fsdp", axis=1, tiled=True),
        lax.all_gather(ffn_gain, "fsdp", axis=0, tiled=True),
        lax.all_gather(w_gate, "fsdp", axis=0, tiled=True),
        lax.all_gather(w_up, "fsdp", axis=0, tiled=True),
        lax.all_gather(w_down, "fsdp", axis=1, tiled=True),
    )
    seq_count, local_len, model_width = tokens.shape
    seq_len = segment_ids.shape[1]
    head_size = full_qgain.shape[0]
    kv_local = full_key.shape[1] // head_size
    heads_local = full_query.shape[1] // head_size
    group_size = heads_local // kv_local
    scale_factor = head_size ** (-0.5)
    index_full = jnp.arange(seq_len, dtype=jnp.int32)[None, :]
    previous = jnp.concatenate([segment_ids[:, :1] - 1, segment_ids[:, :-1]], 1)
    starts = jnp.where(segment_ids != previous, index_full, 0)
    position_full = index_full - lax.cummax(starts, axis=1)
    offset = lax.axis_index("ctx") * local_len
    query_index = offset + jnp.arange(local_len, dtype=jnp.int32)
    query_seg = lax.dynamic_slice_in_dim(segment_ids, offset, local_len, 1)
    query_pos = lax.dynamic_slice_in_dim(position_full, offset, local_len, 1)
    valid = (query_seg != 0).astype(jnp.float32)
    valid_three = valid[:, :, None]
    half_size = head_size // 2
    frequency = rope_base ** (-(jnp.arange(half_size, dtype=jnp.float32) * 2.0 / head_size))
    turned = query_pos.astype(jnp.float32)[:, :, None] * frequency
    cosine = jnp.cos(turned)[:, :, None, :]
    sine = jnp.sin(turned)[:, :, None, :]
    tokens_f = tokens.astype(jnp.float32)
    gain_one = full_attn_gain.astype(jnp.float32)
    gain_two = full_ffn_gain.astype(jnp.float32)
    qgain = full_qgain.astype(jnp.float32)
    kgain = full_kgain.astype(jnp.float32)
    attn_scale = inv_scale(tokens_f)
    normed = (tokens_f * attn_scale * gain_one).astype(jnp.bfloat16)
    query_pre = jnp.einsum(
        "bsd,dh->bsh", normed, full_query, preferred_element_type=jnp.float32
    ).reshape(seq_count, local_len, heads_local, head_size)
    key_pre = jnp.einsum(
        "bsd,dh->bsh", normed, full_key, preferred_element_type=jnp.float32
    ).reshape(seq_count, local_len, kv_local, head_size)
    value_pre = jnp.einsum("bsd,dh->bsh", normed, full_value, preferred_element_type=jnp.float32)
    query_scale = inv_scale(query_pre)
    key_scale = inv_scale(key_pre)
    queries = (
        rotate(query_pre * query_scale * qgain, cosine, sine)
        .astype(jnp.bfloat16)
        .reshape(seq_count, local_len, kv_local, group_size, head_size)
    )
    keys = rotate(key_pre * key_scale * kgain, cosine, sine).astype(jnp.bfloat16)
    values = value_pre.astype(jnp.bfloat16).reshape(seq_count, local_len, kv_local, head_size)

    def allowed_mask(count):
        key_index = jnp.arange(count, dtype=jnp.int32)
        joined = (
            (query_seg[:, :, None] == segment_ids[:, None, :])
            & (key_index[None, None, :] <= query_index[None, :, None])
            & (segment_ids[:, None, :] != 0)
        )
        return joined[:, :, None, None, :]

    stat_shape = (seq_count, local_len, kv_local, group_size)
    run_max = jnp.full(stat_shape, masked_score, jnp.float32)
    piece_keys = lax.all_gather(keys, "ctx", axis=1, tiled=True)
    piece_values = lax.all_gather(values, "ctx", axis=1, tiled=True)
    allowed = allowed_mask(piece_keys.shape[1])
    scores = (
        jnp.einsum("bqkgd,btkd->bqkgt", queries, piece_keys, preferred_element_type=jnp.float32)
        * scale_factor
    )
    masked = jnp.where(allowed, scores, masked_score)
    new_max = jnp.maximum(run_max, jnp.max(masked, -1))
    weights = jnp.where(allowed, jnp.exp(masked - new_max[..., None]), 0.0)
    new_total = jnp.sum(weights, -1)
    new_acc = jnp.einsum(
        "bqkgt,btkd->bqkgd",
        weights.astype(jnp.bfloat16),
        piece_values,
        preferred_element_type=jnp.float32,
    )
    total_safe = jnp.where(query_seg[:, :, None, None] != 0, new_total, 1.0)
    mixed = new_acc / total_safe[..., None] * valid[:, :, None, None, None]
    log_total = new_max + jnp.log(total_safe)
    mixed_low = mixed.astype(jnp.bfloat16)
    out_four = full_out.reshape(kv_local, group_size, head_size, model_width)
    branch_part = jnp.einsum(
        "bqkgd,kgde->bqe", mixed_low, out_four, preferred_element_type=jnp.float32
    )
    branch = lax.psum(branch_part.astype(jnp.bfloat16), "tp").astype(jnp.float32)
    resid = tokens_f + valid_three * branch
    ffn_scale = inv_scale(resid)
    normed_two = (resid * ffn_scale * gain_two).astype(jnp.bfloat16)
    gate = jnp.einsum("bsd,df->bsf", normed_two, full_gate, preferred_element_type=jnp.float32)
    upper = jnp.einsum("bsd,df->bsf", normed_two, full_up, preferred_element_type=jnp.float32)
    sigma = jax.nn.sigmoid(gate)
    silu_gate = gate * sigma
    active = (silu_gate * upper).astype(jnp.bfloat16)
    ffn_part = jnp.einsum("bsf,fd->bsd", active, full_down, preferred_element_type=jnp.float32)
    ffn_out = lax.psum(ffn_part.astype(jnp.bfloat16), "tp").astype(jnp.float32)
    layer_out = (resid + valid_three * ffn_out).astype(jnp.bfloat16)
    back_query, back_key, back_value, back_out, back_gate, back_up, back_down = (
        lax.all_gather(w_query, "fsdp", axis=0, tiled=True),
        lax.all_gather(w_key, "fsdp", axis=0, tiled=True),
        lax.all_gather(w_value, "fsdp", axis=0, tiled=True),
        lax.all_gather(w_out, "fsdp", axis=1, tiled=True),
        lax.all_gather(w_gate, "fsdp", axis=0, tiled=True),
        lax.all_gather(w_up, "fsdp", axis=0, tiled=True),
        lax.all_gather(w_down, "fsdp", axis=1, tiled=True),
    )
    grad_f = out_grad.astype(jnp.float32)
    grad_branch_two = (valid_three * grad_f).astype(jnp.bfloat16)
    down_grad = jnp.einsum(
        "bsf,bsd->fd", active, grad_branch_two, preferred_element_type=jnp.float32
    )
    grad_active = jnp.einsum(
        "bsd,fd->bsf", grad_branch_two, back_down, preferred_element_type=jnp.float32
    )
    grad_gate = (grad_active * upper * sigma * (1.0 + gate * (1.0 - sigma))).astype(jnp.bfloat16)
    grad_upper = (grad_active * silu_gate).astype(jnp.bfloat16)
    gate_grad = jnp.einsum("bsd,bsf->df", normed_two, grad_gate, preferred_element_type=jnp.float32)
    up_grad = jnp.einsum("bsd,bsf->df", normed_two, grad_upper, preferred_element_type=jnp.float32)
    grad_two_part = jnp.einsum(
        "bsf,df->bsd", grad_gate, back_gate, preferred_element_type=jnp.float32
    ) + jnp.einsum("bsf,df->bsd", grad_upper, back_up, preferred_element_type=jnp.float32)
    grad_two = lax.psum(grad_two_part.astype(jnp.bfloat16), "tp").astype(jnp.float32)
    ffn_gain_grad = jnp.sum(grad_two * resid * ffn_scale, (0, 1))
    grad_resid = grad_f + norm_back(resid, ffn_scale, gain_two, grad_two)
    grad_branch = (valid_three * grad_resid).astype(jnp.bfloat16)
    out_weight_grad = jnp.einsum(
        "bqkgd,bqe->kgde", mixed_low, grad_branch, preferred_element_type=jnp.float32
    ).reshape(heads_local * head_size, model_width)
    back_four = back_out.reshape(kv_local, group_size, head_size, model_width)
    grad_mixed = jnp.einsum(
        "bqe,kgde->bqkgd", grad_branch, back_four, preferred_element_type=jnp.float32
    ).astype(jnp.bfloat16)
    delta = jnp.sum(grad_mixed.astype(jnp.float32) * mixed, -1)
    piece_keys = lax.all_gather(keys, "ctx", axis=1, tiled=True)
    piece_values = lax.all_gather(values, "ctx", axis=1, tiled=True)
    count = piece_keys.shape[1]
    allowed = allowed_mask(count)
    scores = (
        jnp.einsum("bqkgd,btkd->bqkgt", queries, piece_keys, preferred_element_type=jnp.float32)
        * scale_factor
    )
    probs = jnp.where(
        allowed,
        jnp.exp(jnp.where(allowed, scores, 0.0) - jnp.where(allowed, log_total[..., None], 0.0)),
        0.0,
    )
    value_term = jnp.einsum(
        "bqkgt,bqkgd->btkd",
        probs.astype(jnp.bfloat16),
        grad_mixed,
        preferred_element_type=jnp.float32,
    )
    grad_probs = jnp.einsum(
        "bqkgd,btkd->bqkgt", grad_mixed, piece_values, preferred_element_type=jnp.float32
    )
    grad_scores = (probs * (grad_probs - delta[..., None])).astype(jnp.bfloat16)
    query_term = (
        jnp.einsum("bqkgt,btkd->bqkgd", grad_scores, piece_keys, preferred_element_type=jnp.float32)
        * scale_factor
    )
    key_term = (
        jnp.einsum("bqkgt,bqkgd->btkd", grad_scores, queries, preferred_element_type=jnp.float32)
        * scale_factor
    )
    key_full = key_term
    value_full = value_term
    grad_query_rot, key_full, value_full = (query_term, key_full, value_full)
    grad_key_rot, grad_value = (
        lax.psum_scatter(
            key_full.astype(jnp.bfloat16), "ctx", scatter_dimension=1, tiled=True
        ).astype(jnp.float32),
        lax.psum_scatter(
            value_full.astype(jnp.bfloat16), "ctx", scatter_dimension=1, tiled=True
        ).astype(jnp.float32),
    )
    grad_query_norm = rotate(
        grad_query_rot.reshape(seq_count, local_len, heads_local, head_size), cosine, -sine
    )
    grad_key_norm = rotate(grad_key_rot, cosine, -sine)
    qgain_part = jnp.sum(grad_query_norm * query_pre * query_scale, (0, 1, 2))
    kgain_part = jnp.sum(grad_key_norm * key_pre * key_scale, (0, 1, 2))
    grad_query_pre = (
        norm_back(query_pre, query_scale, qgain, grad_query_norm)
        .astype(jnp.bfloat16)
        .reshape(seq_count, local_len, heads_local * head_size)
    )
    grad_key_pre = (
        norm_back(key_pre, key_scale, kgain, grad_key_norm)
        .astype(jnp.bfloat16)
        .reshape(seq_count, local_len, kv_local * head_size)
    )
    grad_value_pre = grad_value.astype(jnp.bfloat16).reshape(
        seq_count, local_len, kv_local * head_size
    )
    query_grad = jnp.einsum(
        "bsd,bsh->dh", normed, grad_query_pre, preferred_element_type=jnp.float32
    )
    key_grad = jnp.einsum("bsd,bsh->dh", normed, grad_key_pre, preferred_element_type=jnp.float32)
    value_grad = jnp.einsum(
        "bsd,bsh->dh", normed, grad_value_pre, preferred_element_type=jnp.float32
    )
    grad_one_part = (
        jnp.einsum("bsh,dh->bsd", grad_query_pre, back_query, preferred_element_type=jnp.float32)
        + jnp.einsum("bsh,dh->bsd", grad_key_pre, back_key, preferred_element_type=jnp.float32)
        + jnp.einsum("bsh,dh->bsd", grad_value_pre, back_value, preferred_element_type=jnp.float32)
    )
    grad_one, qgain_grad, kgain_grad = (
        lax.psum(grad_one_part.astype(jnp.bfloat16), "tp").astype(jnp.float32),
        lax.psum(qgain_part.astype(jnp.bfloat16), "tp").astype(jnp.float32),
        lax.psum(kgain_part.astype(jnp.bfloat16), "tp").astype(jnp.float32),
    )
    attn_gain_grad = jnp.sum(grad_one * tokens_f * attn_scale, (0, 1))
    input_grad = grad_resid + norm_back(tokens_f, attn_scale, gain_one, grad_one)
    reduced = (
        lax.psum_scatter(
            attn_gain_grad.astype(jnp.bfloat16), "fsdp", scatter_dimension=0, tiled=True
        ).astype(jnp.float32),
        lax.psum_scatter(
            query_grad.astype(jnp.bfloat16), "fsdp", scatter_dimension=0, tiled=True
        ).astype(jnp.float32),
        lax.psum_scatter(
            key_grad.astype(jnp.bfloat16), "fsdp", scatter_dimension=0, tiled=True
        ).astype(jnp.float32),
        lax.psum_scatter(
            value_grad.astype(jnp.bfloat16), "fsdp", scatter_dimension=0, tiled=True
        ).astype(jnp.float32),
        lax.psum_scatter(
            qgain_grad.astype(jnp.bfloat16), "fsdp", scatter_dimension=0, tiled=True
        ).astype(jnp.float32),
        lax.psum_scatter(
            kgain_grad.astype(jnp.bfloat16), "fsdp", scatter_dimension=0, tiled=True
        ).astype(jnp.float32),
        lax.psum_scatter(
            out_weight_grad.astype(jnp.bfloat16), "fsdp", scatter_dimension=1, tiled=True
        ).astype(jnp.float32),
        lax.psum_scatter(
            ffn_gain_grad.astype(jnp.bfloat16), "fsdp", scatter_dimension=0, tiled=True
        ).astype(jnp.float32),
        lax.psum_scatter(
            gate_grad.astype(jnp.bfloat16), "fsdp", scatter_dimension=0, tiled=True
        ).astype(jnp.float32),
        lax.psum_scatter(
            up_grad.astype(jnp.bfloat16), "fsdp", scatter_dimension=0, tiled=True
        ).astype(jnp.float32),
        lax.psum_scatter(
            down_grad.astype(jnp.bfloat16), "fsdp", scatter_dimension=1, tiled=True
        ).astype(jnp.float32),
    )
    summed = (
        lax.psum(reduced[0].astype(jnp.bfloat16), "ctx").astype(jnp.float32),
        lax.psum(reduced[1].astype(jnp.bfloat16), "ctx").astype(jnp.float32),
        lax.psum(reduced[2].astype(jnp.bfloat16), "ctx").astype(jnp.float32),
        lax.psum(reduced[3].astype(jnp.bfloat16), "ctx").astype(jnp.float32),
        lax.psum(reduced[4].astype(jnp.bfloat16), "ctx").astype(jnp.float32),
        lax.psum(reduced[5].astype(jnp.bfloat16), "ctx").astype(jnp.float32),
        lax.psum(reduced[6].astype(jnp.bfloat16), "ctx").astype(jnp.float32),
        lax.psum(reduced[7].astype(jnp.bfloat16), "ctx").astype(jnp.float32),
        lax.psum(reduced[8].astype(jnp.bfloat16), "ctx").astype(jnp.float32),
        lax.psum(reduced[9].astype(jnp.bfloat16), "ctx").astype(jnp.float32),
        lax.psum(reduced[10].astype(jnp.bfloat16), "ctx").astype(jnp.float32),
    )
    return (
        layer_out,
        input_grad,
        summed[0],
        summed[1],
        summed[2],
        summed[3],
        summed[4],
        summed[5],
        summed[6],
        summed[7],
        summed[8],
        summed[9],
        summed[10],
    )


def solution(mesh):
    placed = (
        P("fsdp", "ctx", None),
        P("fsdp", None),
        P("fsdp"),
        P("fsdp", "tp"),
        P("fsdp", "tp"),
        P("fsdp", "tp"),
        P("fsdp"),
        P("fsdp"),
        P("tp", "fsdp"),
        P("fsdp"),
        P("fsdp", "tp"),
        P("fsdp", "tp"),
        P("tp", "fsdp"),
        P("fsdp", "ctx", None),
    )
    return jax.shard_map(
        body,
        mesh=mesh,
        in_specs=placed,
        out_specs=(
            P("fsdp", "ctx", None),
            P("fsdp", "ctx", None),
            P("fsdp"),
            P("fsdp", "tp"),
            P("fsdp", "tp"),
            P("fsdp", "tp"),
            P("fsdp"),
            P("fsdp"),
            P("tp", "fsdp"),
            P("fsdp"),
            P("fsdp", "tp"),
            P("fsdp", "tp"),
            P("tp", "fsdp"),
        ),
        check_vma=False,
    )
```

profile of v0, /device:TPU:0, one launch (start us, length us, event | category | flops | bytes accessed | tf_op | source)
XLA Modules:
  0.0 928.1 jit_solution(4689510979285144952)
XLA Ops:
  10.2 5.3 all-gather
  17.8 13.3 %all_gather.51 = bf16[1024,256]{0,1:T(8,128)(2,1)S(1)} all-gather(bf16[512,256]{0,1:T(8,128)(2,1)S(1)} %copy.220), channel_id=1, replica_groups=mesh['fsdp'=2,'ctx'=4,'tp'=4] {'fsdp'}, dimensions={0}, use_global_device_ids=true | all-gather | bytes 786432 | tf_op jit(solution)/shard_map/all_gather | solution.py:60
  39.6 5.4 all-reduce.11
  52.8 7.1 all_gather.49
  63.8 4.2 and_and_fusion
  74.9 24.4 %all-gather.12.cloned.1.call-done = bf16[2,2048,2,128]{3,1,2,0:T(8,128)(2,1)} async-done(((bf16[2,512,2,128]{3,1,2,0:T(8,128)(2,1)}), bf16[2,2048,2,128]{3,1,2,0:T(8,128)(2,1)}) %all-gather.12.cloned.1.call-update) | async-done | bytes 2097168 | tf_op jit(solution)/shard_map/all_gather | solution.py:127
  99.3 16.5 %fusion.5 = (f32[2,512,2,2]{1,3,2,0:T(2,128)S(1)}, f32[2,2,2048,512,2]{3,2,4,1,0:T(8,128)}) fusion(pred[2,512,2048]{1,2,0:T(8,128)(4,1)} %and_and_fusion, bf16[2,512,2,2,64]{4,1,3,2,0:T(8,128)(2,1)} %bitcast.292, bf16[2,512,2,2,64]{4,1,3,2,0:T(8,128)(2,1)} %bitcast.290, bf16[2,2048,2,128]{3,1,2,0:T(8,128)(2,1)} %all-gather.12.cloned.1.call-done), kind=kOutput, calls=%fused_computation.9 | convolution fusion | flops 2174742528 | bytes 38813696 | tf_op jit(solution)/shard_map/bqkgd,btkd->bqkgt/dot_general | solution.py:131
  115.8 15.0 %fusion.6 = f32[2,512,2,2]{1,3,2,0:T(2,128)S(1)} fusion(f32[2,2,2048,512,2]{3,2,4,1,0:T(8,128)} %get-tuple-element.74, f32[2,512,2,2]{1,3,2,0:T(2,128)S(1)} %broadcast_maximum_fusion, pred[2,512,2048]{1,2,0:T(8,128)(4,1)S(1)} %copy-done.7), kind=kLoop, calls=%fused_computation.10 | loop fusion | flops 41938944 | bytes 35684352 | tf_op jit(solution)/shard_map/reduce_sum | solution.py:137
  130.9 15.0 %all-gather.10.cloned.1.call-done = bf16[2,2048,2,128]{1,3,2,0:T(8,128)(2,1)} async-done(((bf16[2,512,2,128]{1,3,2,0:T(8,128)(2,1)}), bf16[2,2048,2,128]{1,3,2,0:T(8,128)(2,1)}) %all-gather.10.cloned.1.call-update) | async-done | bytes 2097168 | tf_op jit(solution)/shard_map/all_gather | solution.py:128
  145.9 18.1 %fusion.114 = (bf16[2,512,2,2,128]{1,4,3,2,0:T(8,128)(2,1)S(1)}, f32[2,512,2,2,128]{1,4,3,2,0:T(8,128)}) fusion(f32[2,512]{1,0:T(2,128)S(1)} %get-tuple-element.42, f32[2,512,2,2]{1,3,2,0:T(2,128)S(1)} %get-tuple-element.41, f32[2,2,2048,512,2]{3,2,4,1,0:T(8,128)} %get-tuple-element.74, f32[2,512,2,2]{1,3,2,0:T(2,128)S(1)} %broadcast_maximum_fusion, ...), kind=kOutput, calls=%fused_computation.193 | convolution fusion | flops 2190999552 | bytes 40931328 | tf_op jit(solution)/shard_map/bqkgt,btkd->bqkgd/dot_general | solution.py:138
  164.0 3.4 all-gather.16.cloned.1.call-done
  167.4 3.8 bitcast_convert_fusion
  173.5 4.4 all-gather.1
  177.8 45.0 %all-reduce.17.cloned.1.call-done = bf16[2,512,1024]{2,1,0:T(8,128)(2,1)} async-done(((bf16[2,512,1024]{2,1,0:T(8,128)(2,1)}), bf16[2,512,1024]{2,1,0:T(8,128)(2,1)}) %all-reduce.17.cloned.1.call-update) | async-done | bytes 2097168 | tf_op jit(solution)/shard_map/psum | solution.py:152
  227.9 23.7 %all-gather.20.cloned.1.call-done = bf16[1024,768]{1,0:T(8,128)(2,1)} async-done(((bf16[512,768]{1,0:T(8,128)(2,1)}), bf16[1024,768]{1,0:T(8,128)(2,1)}) %all-gather.20.cloned.1.call-update) | async-done | bytes 1572880 | tf_op jit(solution)/shard_map/all_gather | solution.py:67
  251.5 5.5 fusion.70
  257.0 23.3 %all-gather.18.cloned.1.call-done = bf16[1024,768]{1,0:T(8,128)(2,1)} async-done(((bf16[512,768]{1,0:T(8,128)(2,1)}), bf16[1024,768]{1,0:T(8,128)(2,1)}) %all-gather.18.cloned.1.call-update) | async-done | bytes 1572880 | tf_op jit(solution)/shard_map/all_gather | solution.py:66
  280.3 5.5 fusion.74
  285.8 23.3 %all-gather.22.cloned.1.call-done = bf16[768,1024]{1,0:T(8,128)(2,1)} async-done(((bf16[768,512]{1,0:T(8,128)(2,1)}), bf16[768,1024]{1,0:T(8,128)(2,1)}) %all-gather.22.cloned.1.call-update) | async-done | bytes 1572880 | tf_op jit(solution)/shard_map/all_gather | solution.py:68
  309.0 8.0 multiply_convert_fusion.2
  319.6 3.2 add_convert_fusion.1
  322.8 51.5 %all-reduce.19.cloned.1.call-done = bf16[2,512,1024]{2,1,0:T(8,128)(2,1)} async-done(((bf16[2,512,1024]{2,1,0:T(8,128)(2,1)}), bf16[2,512,1024]{2,1,0:T(8,128)(2,1)}) %all-reduce.19.cloned.1.call-update) | async-done | bytes 2097168 | tf_op jit(solution)/shard_map/psum | solution.py:188
  374.3 4.2 fusion.29
  378.7 4.5 multiply_reduce_fusion.2
  384.1 21.8 %fusion.1 = bf16[2,512,2,2,2048]{1,4,3,2,0:T(8,128)(2,1)} fusion(f32[2,2,2048,512,2]{3,2,4,1,0:T(8,128)} %get-tuple-element.74, f32[2,512,2,2]{1,3,2,0:T(2,128)S(1)} %get-tuple-element.77, f32[2,512,2,2]{1,3,2,0:T(2,128)S(1)} %get-tuple-element.40, pred[2,512,2048]{1,2,0:T(8,128)(4,1)S(1)} %copy-done.8, ...), kind=kOutput, calls=%fused_computation.2 | convolution fusion | flops 2214592512 | bytes 55607296 | tf_op jit(solution)/shard_map/bqkgd,btkd->bqkgt/dot_general | solution.py:219
  406.0 11.7 %fusion.38 = bf16[2,2048,2,128]{3,1,2,0:T(8,128)(2,1)} fusion(bf16[2,512,2,2,2048]{1,4,3,2,0:T(8,128)(2,1)} %fusion.1, bf16[2,512,2,2,64]{4,1,3,2,0:T(8,128)(2,1)S(1)} %bitcast.293, bf16[2,512,2,2,64]{4,1,3,2,0:T(8,128)(2,1)S(1)} %bitcast.291), kind=kOutput, calls=%fused_computation.76 | convolution fusion | flops 2151677952 | bytes 19922944 | tf_op jit(solution)/shard_map/bqkgt,bqkgd->btkd/dot_general | solution.py:228
  417.8 19.0 %fusion.39 = bf16[2,2048,2,128]{1,3,2,0:T(8,128)(2,1)} fusion(bf16[2,512,2,2,128]{1,4,3,2,0:T(8,128)(2,1)} %copy-done.57, f32[2,2,2048,512,2]{3,2,4,1,0:T(8,128)} %get-tuple-element.74, f32[2,512,2,2]{1,3,2,0:T(2,128)S(1)} %get-tuple-element.40, pred[2,512,2048]{1,2,0:T(8,128)(4,1)} %and_and_fusion), kind=kOutput, calls=%fused_computation.77 | convolution fusion | flops 2198863872 | bytes 38813696 | tf_op jit(solution)/shard_map/bqkgt,bqkgd->btkd/dot_general | solution.py:213
  436.9 5.5 fusion.46
  443.6 5.1 bitcast_convert_fusion.4
  448.8 5.0 bitcast_convert_fusion.3
  454.1 9.1 fusion.64
  470.0 5.2 bitcast_convert_fusion.2
  486.8 5.1 convolution_convert_fusion
  491.8 15.5 %reduce-scatter.12.cloned.1.call-done = bf16[2,512,2,128]{1,3,2,0:T(8,128)(2,1)} async-done(((bf16[2,2048,2,128]{1,3,2,0:T(8,128)(2,1)}), bf16[2,512,2,128]{1,3,2,0:T(8,128)(2,1)}) %reduce-scatter.12.cloned.1.call-update) | async-done | bytes 524304 | tf_op jit(solution)/shard_map/reduce_scatter | solution.py:238
  516.4 12.6 %reduce-scatter.20.cloned.1.call-done = bf16[512,512]{1,0:T(8,128)(2,1)} async-done(((bf16[512,1024]{1,0:T(8,128)(2,1)}), bf16[512,512]{1,0:T(8,128)(2,1)}) %reduce-scatter.20.cloned.1.call-update) | async-done | bytes 524304 | tf_op jit(solution)/shard_map/reduce_scatter | solution.py:299
  529.0 29.0 %reduce-scatter.22.cloned.1.call-done = bf16[512,768]{1,0:T(8,128)(2,1)} async-done(((bf16[1024,768]{1,0:T(8,128)(2,1)}), bf16[512,768]{1,0:T(8,128)(2,1)}) %reduce-scatter.22.cloned.1.call-update) | async-done | bytes 786448 | tf_op jit(solution)/shard_map/reduce_scatter | solution.py:305
  558.0 28.9 %reduce-scatter.24.cloned.1.call-done = bf16[512,768]{1,0:T(8,128)(2,1)} async-done(((bf16[1024,768]{1,0:T(8,128)(2,1)}), bf16[512,768]{1,0:T(8,128)(2,1)}) %reduce-scatter.24.cloned.1.call-update) | async-done | bytes 786448 | tf_op jit(solution)/shard_map/reduce_scatter | solution.py:308
  586.9 22.5 %reduce-scatter.14.cloned.1.call-done = bf16[512,512]{1,0:T(8,128)(2,1)} async-done(((bf16[1024,512]{1,0:T(8,128)(2,1)}), bf16[512,512]{1,0:T(8,128)(2,1)}) %reduce-scatter.14.cloned.1.call-update) | async-done | bytes 524304 | tf_op jit(solution)/shard_map/reduce_scatter | solution.py:284
  609.4 28.3 %reduce-scatter.26.cloned.1.call-done = bf16[768,512]{1,0:T(8,128)(2,1)} async-done(((bf16[768,1024]{1,0:T(8,128)(2,1)}), bf16[768,512]{1,0:T(8,128)(2,1)}) %reduce-scatter.26.cloned.1.call-update) | async-done | bytes 786448 | tf_op jit(solution)/shard_map/reduce_scatter | solution.py:311
  637.7 17.3 %reduce-scatter.16.cloned.1.call-done = bf16[512,256]{1,0:T(8,128)(2,1)} async-done(((bf16[1024,256]{1,0:T(8,128)(2,1)}), bf16[512,256]{1,0:T(8,128)(2,1)}) %reduce-scatter.16.cloned.1.call-update) | async-done | bytes 262160 | tf_op jit(solution)/shard_map/reduce_scatter | solution.py:287
  655.0 17.3 %reduce-scatter.18.cloned.1.call-done = bf16[512,256]{1,0:T(8,128)(2,1)} async-done(((bf16[1024,256]{1,0:T(8,128)(2,1)}), bf16[512,256]{1,0:T(8,128)(2,1)}) %reduce-scatter.18.cloned.1.call-update) | async-done | bytes 262160 | tf_op jit(solution)/shard_map/reduce_scatter | solution.py:290
  673.7 87.2 %all-reduce.21.cloned.1.call-done = (bf16[2,512,1024]{2,1,0:T(8,128)(2,1)}, bf16[2,512,1024]{2,1,0:T(8,128)(2,1)}) async-done(((bf16[2,512,1024]{2,1,0:T(8,128)(2,1)}, bf16[2,512,1024]{2,1,0:T(8,128)(2,1)}), (bf16[2,512,1024]{2,1,0:T(8,128)(2,1)}, bf16[2,512,1024]{2,1,0:T(8,128)(2,1)})) %all-reduce.21.cloned.1.call-update) | async-done | bytes 4194320 | tf_op jit(solution)/shard_map/psum | solution.py:162
  760.9 3.4 fusion.33
  764.4 5.0 all-reduce.10
  769.7 6.0 all-reduce.6
  775.7 12.3 %all-reduce.8 = (bf16[512]{0:T(512)(128)(2,1)S(1)}, bf16[64]{0:T(256)(128)(2,1)S(1)}, bf16[64]{0:T(256)(128)(2,1)S(1)}, bf16[512]{0:T(512)(128)(2,1)S(1)}) all-reduce(bf16[512]{0:T(512)(128)(2,1)S(1)} %dynamic-slice.3, bf16[64]{0:T(256)(128)(2,1)S(1)} %get-tuple-element.17, ...), channel_id=1, replica_groups=mesh['fsdp'=2,'ctx'=4,'tp'=4] {'ctx'}, use_global_device_ids=true, to_apply=%region_21.22 | all-reduce | flops 1152 | bytes 4608 | tf_op jit(solution)/shard_map/psum | solution.py:316
  790.2 8.0 fusion.24
  798.2 112.6 %all-reduce.23.cloned.1.call-done = (bf16[512,512]{1,0:T(8,128)(2,1)}, bf16[512,256]{1,0:T(8,128)(2,1)}, bf16[512,256]{1,0:T(8,128)(2,1)}, bf16[512,512]{1,0:T(8...) async-done(((bf16[512,512]{1,0:T(8,128)(2,1)}, bf16[512,256]{1,0:T(8,128)(2,1)}, bf16[512,256]{1,0:T(8,128)(2,1)}, ...) | async-done | bytes 3932176 | tf_op jit(solution)/shard_map/psum | solution.py:317
  (249 shorter events, 83.7 us)
Async XLA Ops:
  7.2 25.1 %copy-start = (bf16[2,512,1024]{2,1,0:T(8,128)(2,1)S(1)}, bf16[2,512,1024]{2,1,0:T(8,128)(2,1)}, u32[]{:S(2)}) copy-start(bf16[2,512,1024]{2,1,0:T(8,128)(2,1)} %param.14) | copy-start | bytes 6291460
  7.2 10.4 %copy-start.32 = (bf16[512,256]{1,0:T(8,128)(2,1)S(1)}, bf16[512,256]{1,0:T(8,128)(2,1)}, u32[]{:S(2)}) copy-start(bf16[512,256]{1,0:T(8,128)(2,1)} %param.18) | copy-start | bytes 786436
  7.2 23.9 %copy-start.29 = (s32[2,2048]{1,0:T(2,128)S(1)}, s32[2,2048]{1,0:T(2,128)}, u32[]{:S(2)}) copy-start(s32[2,2048]{1,0:T(2,128)} %param.15) | copy-start | bytes 49156
  7.2 60.8 %all-gather.14.cloned.1.call-start = ((), (), s32[]{:S(2)}) async-start(), calls=%async_computation.11 | async-start | bytes 1572864 | tf_op jit(solution)/shard_map/all_gather | solution.py:59
  9.5 89.8 %all-gather.12.cloned.1.call-start = ((), (), s32[]{:S(2)}) async-start(), calls=%async_computation.10 | async-start | bytes 2621440 | tf_op jit(solution)/shard_map/all_gather | solution.py:127
  15.5 52.5 %copy-start.37 = (f32[2,1,512]{2,1,0:T(1,128)}, f32[2,1,512]{2,1,0:T(1,128)S(1)}, u32[]{:S(2)}) copy-start(f32[2,1,512]{2,1,0:T(1,128)S(1)} %convert_element_type.277) | copy-start | bytes 12292
  17.6 50.4 %copy-start.39 = (f32[2,512]{1,0:T(2,128)}, f32[2,512]{1,0:T(2,128)S(1)}, u32[]{:S(2)}) copy-start(f32[2,512]{1,0:T(2,128)S(1)} %add_rsqrt_fusion.3) | copy-start | bytes 12292
  31.1 4.9 copy-start.16
  32.3 5.4 copy-start.45
  32.3 6.8 copy-start.51
  32.3 7.0 copy-start.52
  36.0 35.2 %copy-start.10 = (f32[2,512,64]{1,2,0:T(8,128)}, f32[2,512,64]{1,2,0:T(8,128)S(1)}, u32[]{:S(2)}) copy-start(f32[2,512,64]{1,2,0:T(8,128)S(1)} %get-tuple-element.66) | copy-start | bytes 786436
  37.7 12.8 %copy-start.5 = (f32[2,512,2,128]{3,1,2,0:T(8,128)}, f32[2,512,2,128]{3,1,2,0:T(8,128)S(1)}, u32[]{:S(2)}) copy-start(f32[2,512,2,128]{3,1,2,0:T(8,128)S(1)} %copy.221) | copy-start | bytes 3145732
  45.0 5.6 copy-start.43
  51.7 94.3 %all-gather.10.cloned.1.call-start = ((), (), s32[]{:S(2)}) async-start(), calls=%async_computation.9 | async-start | bytes 2621440 | tf_op jit(solution)/shard_map/all_gather | solution.py:128
  62.3 105.1 %all-gather.16.cloned.1.call-start = ((), (), s32[]{:S(2)}) async-start(), calls=%async_computation.12 | async-start | bytes 1572864 | tf_op jit(solution)/shard_map/all_gather | solution.py:64
  62.9 160.0 %all-reduce.17.cloned.1.call-start = ((), (), s32[]{:S(2)}) async-start(), calls=%async_computation.13 | async-start | bytes 4194304 | tf_op jit(solution)/shard_map/psum | solution.py:152
  63.0 7.7 copy-start.41
  99.3 16.6 %copy-start.7 = (pred[2,512,2048]{1,2,0:T(8,128)(4,1)S(1)}, pred[2,512,2048]{1,2,0:T(8,128)(4,1)}, u32[]{:S(2)}) copy-start(pred[2,512,2048]{1,2,0:T(8,128)(4,1)} %and_and_fusion) | copy-start | bytes 6291460
  164.0 7.3 copy-start.53
  171.3 80.2 %all-gather.20.cloned.1.call-start = ((), (), s32[]{:S(2)}) async-start(), calls=%async_computation.15 | async-start | bytes 2359296 | tf_op jit(solution)/shard_map/all_gather | solution.py:67
  171.9 108.4 %all-gather.18.cloned.1.call-start = ((), (), s32[]{:S(2)}) async-start(), calls=%async_computation.14 | async-start | bytes 2359296 | tf_op jit(solution)/shard_map/all_gather | solution.py:66
  172.6 136.4 %all-gather.22.cloned.1.call-start = ((), (), s32[]{:S(2)}) async-start(), calls=%async_computation.16 | async-start | bytes 2359296 | tf_op jit(solution)/shard_map/all_gather | solution.py:68
  173.4 200.9 %all-reduce.19.cloned.1.call-start = ((), (), s32[]{:S(2)}) async-start(), calls=%async_computation.17 | async-start | bytes 4194304 | tf_op jit(solution)/shard_map/psum | solution.py:188
  309.0 8.0 copy-start.49
  322.8 55.8 %copy-start.50 = (bf16[512,1024]{1,0:T(8,128)(2,1)S(1)}, bf16[512,1024]{1,0:T(8,128)(2,1)}, u32[]{:S(2)}) copy-start(bf16[512,1024]{1,0:T(8,128)(2,1)} %all-gather.16.cloned.1.call-done) | copy-start | bytes 3145732
  322.8 153.5 %reduce-scatter.10.cloned.1.call-start = ((), (), s32[]{:S(2)}) async-start(), calls=%async_computation.18 | async-start | bytes 2621440 | tf_op jit(solution)/shard_map/reduce_scatter | solution.py:235
  378.6 5.5 copy-start.8
  378.6 5.5 copy-start.47
  384.1 21.9 %copy-start.23 = (bf16[2,512,4,64]{3,1,2,0:T(8,128)(2,1)S(1)}, bf16[2,512,4,64]{3,1,2,0:T(8,128)(2,1)}, u32[]{:S(2)}) copy-start(bf16[2,512,4,64]{3,1,2,0:T(8,128)(2,1)} %copy.225) | copy-start | bytes 1572868
  384.1 21.9 %copy-start.24 = (bf16[2,512,4,64]{3,1,2,0:T(8,128)(2,1)S(1)}, bf16[2,512,4,64]{3,1,2,0:T(8,128)(2,1)}, u32[]{:S(2)}) copy-start(bf16[2,512,4,64]{3,1,2,0:T(8,128)(2,1)} %copy.226) | copy-start | bytes 1572868
  417.7 19.1 %copy-start.54 = (bf16[2,512,2,2,128]{1,4,3,2,0:T(8,128)(2,1)S(1)}, bf16[2,512,2,2,128]{1,4,3,2,0:T(8,128)(2,1)}, u32[]{:S(2)}) copy-start(bf16[2,512,2,2,128]{1,4,3,2,0:T(8,128)(2,1)} %copy-done.53) | copy-start | bytes 3145732
  417.7 89.6 %reduce-scatter.12.cloned.1.call-start = ((), (), s32[]{:S(2)}) async-start(), calls=%async_computation.19 | async-start | bytes 2621440 | tf_op jit(solution)/shard_map/reduce_scatter | solution.py:238
  436.8 92.2 %reduce-scatter.20.cloned.1.call-start = ((), (), s32[]{:S(2)}) async-start(), calls=%async_computation.23 | async-start | bytes 1572864 | tf_op jit(solution)/shard_map/reduce_scatter | solution.py:299
  443.5 114.5 %reduce-scatter.22.cloned.1.call-start = ((), (), s32[]{:S(2)}) async-start(), calls=%async_computation.24 | async-start | bytes 2359296 | tf_op jit(solution)/shard_map/reduce_scatter | solution.py:305
  448.7 5.4 copy-start.42
  448.7 138.2 %reduce-scatter.24.cloned.1.call-start = ((), (), s32[]{:S(2)}) async-start(), calls=%async_computation.25 | async-start | bytes 2359296 | tf_op jit(solution)/shard_map/reduce_scatter | solution.py:308
  453.9 155.5 %reduce-scatter.14.cloned.1.call-start = ((), (), s32[]{:S(2)}) async-start(), calls=%async_computation.20 | async-start | bytes 1572864 | tf_op jit(solution)/shard_map/reduce_scatter | solution.py:284
  454.1 9.1 copy-start.11
  454.1 9.1 copy-start.15
  469.9 167.7 %reduce-scatter.26.cloned.1.call-start = ((), (), s32[]{:S(2)}) async-start(), calls=%async_computation.26 | async-start | bytes 2359296 | tf_op jit(solution)/shard_map/reduce_scatter | solution.py:311
  470.0 6.3 copy-start.44
  475.2 179.8 %reduce-scatter.16.cloned.1.call-start = ((), (), s32[]{:S(2)}) async-start(), calls=%async_computation.21 | async-start | bytes 786432 | tf_op jit(solution)/shard_map/reduce_scatter | solution.py:287
  486.5 185.8 %reduce-scatter.18.cloned.1.call-start = ((), (), s32[]{:S(2)}) async-start(), calls=%async_computation.22 | async-start | bytes 786432 | tf_op jit(solution)/shard_map/reduce_scatter | solution.py:290
  510.2 250.7 %all-reduce.21.cloned.1.call-start = ((), (), s32[]{:S(2)}) async-start(), calls=%async_computation.27 | async-start | bytes 8388608 | tf_op jit(solution)/shard_map/psum | solution.py:162
  516.4 394.5 %all-reduce.23.cloned.1.call-start = ((), (), s32[]{:S(2)}) async-start(), calls=%async_computation.28 | async-start | bytes 7864320 | tf_op jit(solution)/shard_map/psum | solution.py:317
  910.8 4.9 copy-start.25
  910.8 6.3 copy-start.28
  (30 other events, 66.8 us)
Sparse Core Ops, SparseCore 0:
  10.1 26.9 all-gather.13
  51.8 47.4 all-gather.11
  101.4 44.4 all-gather.9
  147.3 20.0 all-gather.15
  171.4 51.3 all-reduce.16
  224.2 27.2 all-gather.19
  253.1 27.1 all-gather.17
  281.8 27.1 all-gather.21
  322.9 51.3 all-reduce.18
  417.9 43.6 reduce-scatter.9
  464.5 42.8 reduce-scatter.11
  509.4 19.5 reduce-scatter.19
  531.8 26.1 reduce-scatter.21
  560.7 26.1 reduce-scatter.23
  589.0 20.3 reduce-scatter.13
  611.5 26.1 reduce-scatter.25
  640.3 14.6 reduce-scatter.15
  657.7 14.6 reduce-scatter.17
  675.3 85.5 all-reduce.20
  763.7 147.0 all-reduce.22
where the time goes:
time: 935 us; the launch traced here: 928 us
  waiting for transfers between devices  583 us (62%)
  matrix products  173 us (19%)
  other arithmetic  69.9 us (7%)
  blocking collectives  58.7 us (6%)
  local copies, waits for them, and re-layouts  24.3 us (3%)
  between operations  17.4 us (2%)
    psum x1, waiting for transfers between devices, body(): lax.psum(reduced[1].astype(jnp.bfloat16), 'ctx').astype(jnp.float32)  113 us
    psum x1, waiting for transfers between devices, body(): ffn_out = lax.psum(ffn_part.astype(jnp.bfloat16), 'tp').astype(jnp.float32)  87.2 us
    psum x1, waiting for transfers between devices, body(): lax.psum(grad_two_part.astype(jnp.bfloat16), 'tp').astype(jnp.float32)  51.5 us
    psum x1, waiting for transfers between devices, body(): lax.psum(branch_part.astype(jnp.bfloat16), 'tp').astype(jnp.float32)  45 us
    reduce_scatter x1, waiting for transfers between devices, body(): lax.psum_scatter(gate_grad.astype(jnp.bfloat16), 'fsdp', scatter_dimensio...  29 us
    reduce_scatter x1, waiting for transfers between devices, body(): lax.psum_scatter(up_grad.astype(jnp.bfloat16), 'fsdp', scatter_dimension=...  28.9 us
    reduce_scatter x1, waiting for transfers between devices, body(): lax.psum_scatter(down_grad.astype(jnp.bfloat16), 'fsdp', scatter_dimensio...  28.3 us
    all_gather x1, waiting for transfers between devices, body(): piece_keys = lax.all_gather(keys, 'ctx', axis=1, tiled=True)  24.4 us
  transfers between devices with their start and end apart: 20, of which 18 were waited for; matrix products, arithmetic and copies ran while one was open for 20% of the time, Pallas kernels for 0%

commit v1 on v0

--- a/solution.py
+++ b/solution.py
@@ -124,8 +124,11 @@
 
     stat_shape = (seq_count, local_len, kv_local, group_size)
     run_max = jnp.full(stat_shape, masked_score, jnp.float32)
-    piece_keys = lax.all_gather(keys, "ctx", axis=1, tiled=True)
-    piece_values = lax.all_gather(values, "ctx", axis=1, tiled=True)
+    piece_keys, piece_values = jnp.split(
+        lax.all_gather(jnp.concatenate([keys, values], axis=0), "ctx", axis=1, tiled=True),
+        [keys.shape[0]],
+        axis=0,
+    )
     allowed = allowed_mask(piece_keys.shape[1])
     scores = (
         jnp.einsum("bqkgd,btkd->bqkgt", queries, piece_keys, preferred_element_type=jnp.float32)

time: 935 us -> 1040 us (1.11)
  waiting for transfers between devices: 583 us -> 658 us
  matrix products: 173 us -> 194 us
    all_gather x0 -> x1, waiting for transfers between devices: none -> 66.9 us  [body(): lax.all_gather(jnp.concatenate([keys, values], axis=0), 'ctx', axis=1, ti...]
    all_gather x1, waiting for transfers between devices: 15 us -> 37.5 us  [body(): piece_values = lax.all_gather(values, 'ctx', axis=1, tiled=True)]
    dot_general x1 -> x2, matrix products: 16.5 us -> 34.3 us  [body(): jnp.einsum('bqkgd,btkd->bqkgt', queries, piece_keys, preferred_element_ty...]
    psum x1, waiting for transfers between devices: 51.5 us -> 35.1 us  [body(): lax.psum(grad_two_part.astype(jnp.bfloat16), 'tp').astype(jnp.float32)]
  transfers between devices with their start and end apart: 20 -> 21, of which waited for: 18 -> 18; matrix products, arithmetic and copies ran while one was open for 20% -> 23% of each run, Pallas kernels for 0% -> 0%
where the time goes in v1:
time: 1040 us; the launch traced here: 1030 us
  waiting for transfers between devices  658 us (63%)
  matrix products  194 us (19%)
  other arithmetic  72 us (7%)
  blocking collectives  61.6 us (6%)
  local copies, waits for them, and re-layouts  27.3 us (3%)
  between operations  17.4 us (2%)
    psum x1, waiting for transfers between devices, body(): lax.psum(reduced[1].astype(jnp.bfloat16), 'ctx').astype(jnp.float32)  112 us
    psum x1, waiting for transfers between devices, body(): ffn_out = lax.psum(ffn_part.astype(jnp.bfloat16), 'tp').astype(jnp.float32)  87.1 us
    all_gather x1, waiting for transfers between devices, body(): lax.all_gather(jnp.concatenate([keys, values], axis=0), 'ctx', axis=1, ti...  66.9 us
    psum x1, waiting for transfers between devices, body(): lax.psum(branch_part.astype(jnp.bfloat16), 'tp').astype(jnp.float32)  42.7 us
    all_gather x1, waiting for transfers between devices, body(): piece_values = lax.all_gather(values, 'ctx', axis=1, tiled=True)  37.5 us
    psum x1, waiting for transfers between devices, body(): lax.psum(grad_two_part.astype(jnp.bfloat16), 'tp').astype(jnp.float32)  35.1 us
    dot_general x2, matrix products, body(): jnp.einsum('bqkgd,btkd->bqkgt', queries, piece_keys, preferred_element_ty...  34.3 us
    all_gather x1, waiting for transfers between devices, body(): piece_keys = lax.all_gather(keys, 'ctx', axis=1, tiled=True)  33.2 us
  transfers between devices with their start and end apart: 21, of which 18 were waited for; matrix products, arithmetic and copies ran while one was open for 23% of the time, Pallas kernels for 0%

profile of v1, /device:TPU:0, one launch (start us, length us, event | category | flops | bytes accessed | tf_op | source)
XLA Modules:
  0.0 1032.1 jit_solution(2805680222891383135)
XLA Ops:
  10.2 5.3 all-gather
  17.8 13.3 %all_gather.50 = bf16[1024,256]{0,1:T(8,128)(2,1)S(1)} all-gather(bf16[512,256]{0,1:T(8,128)(2,1)S(1)} %copy.229), channel_id=1, replica_groups=mesh['fsdp'=2,'ctx'=4,'tp'=4] {'fsdp'}, dimensions={0}, use_global_device_ids=true | all-gather | bytes 786432 | tf_op jit(solution)/shard_map/all_gather | solution.py:60
  32.4 10.1 all_gather.52
  51.4 4.9 all-reduce.11
  67.8 4.3 and_and_fusion
  81.7 66.9 %all-gather.11.cloned.1.call-done = bf16[4,2048,2,128]{3,1,2,0:T(8,128)(2,1)} async-done(((bf16[4,512,2,128]{3,1,2,0:T(8,128)(2,1)}), bf16[4,2048,2,128]{3,1,2,0:T(8,128)(2,1)}) %all-gather.11.cloned.1.call-update) | async-done | bytes 4194320 | tf_op jit(solution)/shard_map/all_gather | solution.py:128
  148.6 16.3 %fusion.5 = (f32[2,512,2,2]{1,3,2,0:T(2,128)S(1)}, f32[2,2,2048,512,2]{3,2,4,1,0:T(8,128)}) fusion(pred[2,512,2048]{1,2,0:T(8,128)(4,1)} %and_and_fusion, bf16[2,512,2,2,64]{4,1,3,2,0:T(8,128)(2,1)} %bitcast.297, bf16[2,512,2,2,64]{4,1,3,2,0:T(8,128)(2,1)S(1)} %bitcast.294, bf16[4,2048,2,128]{3,1,2,0:T(8,128)(2,1)} %all-gather.11.cloned.1.call-done), kind=kOutput, calls=%fused_computation.9 | convolution fusion | flops 2174742528 | bytes 39337984 | tf_op jit(solution)/shard_map/bqkgd,btkd->bqkgt/dot_general | solution.py:134
  164.9 14.9 %fusion.6 = f32[2,512,2,2]{1,3,2,0:T(2,128)S(1)} fusion(f32[2,2,2048,512,2]{3,2,4,1,0:T(8,128)} %get-tuple-element.74, f32[2,512,2,2]{1,3,2,0:T(2,128)S(1)} %broadcast_maximum_fusion, pred[2,512,2048]{1,2,0:T(8,128)(4,1)S(1)} %copy-done.7), kind=kLoop, calls=%fused_computation.10 | loop fusion | flops 41938944 | bytes 35684352 | tf_op jit(solution)/shard_map/reduce_sum | solution.py:140
  179.8 17.2 %fusion.110 = (bf16[2,512,2,2,128]{1,4,3,2,0:T(8,128)(2,1)S(1)}, f32[2,512,2,2,128]{1,4,3,2,0:T(8,128)}) fusion(f32[2,512]{1,0:T(2,128)S(1)} %get-tuple-element.42, f32[2,512,2,2]{1,3,2,0:T(2,128)S(1)} %get-tuple-element.41, f32[2,2,2048,512,2]{3,2,4,1,0:T(8,128)} %get-tuple-element.74, f32[2,512,2,2]{1,3,2,0:T(2,128)S(1)} %broadcast_maximum_fusion, ...), kind=kOutput, calls=%fused_computation.194 | convolution fusion | flops 2190999552 | bytes 40931328 | tf_op jit(solution)/shard_map/bqkgt,btkd->bqkgd/dot_general | solution.py:141
  198.0 3.8 bitcast_convert_fusion
  205.0 4.4 all-gather.1
  209.4 42.7 %all-reduce.17.cloned.1.call-done = bf16[2,512,1024]{2,1,0:T(8,128)(2,1)} async-done(((bf16[2,512,1024]{2,1,0:T(8,128)(2,1)}), bf16[2,512,1024]{2,1,0:T(8,128)(2,1)}) %all-reduce.17.cloned.1.call-update) | async-done | bytes 2097168 | tf_op jit(solution)/shard_map/psum | solution.py:155
  257.2 23.6 %all-gather.19.cloned.1.call-done = bf16[1024,768]{1,0:T(8,128)(2,1)} async-done(((bf16[512,768]{1,0:T(8,128)(2,1)}), bf16[1024,768]{1,0:T(8,128)(2,1)}) %all-gather.19.cloned.1.call-update) | async-done | bytes 1572880 | tf_op jit(solution)/shard_map/all_gather | solution.py:67
  280.7 5.5 fusion.68
  286.2 23.2 %all-gather.17.cloned.1.call-done = bf16[1024,768]{1,0:T(8,128)(2,1)} async-done(((bf16[512,768]{1,0:T(8,128)(2,1)}), bf16[1024,768]{1,0:T(8,128)(2,1)}) %all-gather.17.cloned.1.call-update) | async-done | bytes 1572880 | tf_op jit(solution)/shard_map/all_gather | solution.py:66
  309.4 5.5 fusion.72
  314.9 23.3 %all-gather.21.cloned.1.call-done = bf16[768,1024]{1,0:T(8,128)(2,1)} async-done(((bf16[768,512]{1,0:T(8,128)(2,1)}), bf16[768,1024]{1,0:T(8,128)(2,1)}) %all-gather.21.cloned.1.call-update) | async-done | bytes 1572880 | tf_op jit(solution)/shard_map/all_gather | solution.py:68
  338.1 8.0 multiply_convert_fusion.2
  352.8 33.2 %all-gather.23.cloned.1.call-done = bf16[2,2048,2,128]{3,1,2,0:T(8,128)(2,1)} async-done(((bf16[2,512,2,128]{3,1,2,0:T(8,128)(2,1)}), bf16[2,2048,2,128]{3,1,2,0:T(8,128)(2,1)}) %all-gather.23.cloned.1.call-update) | async-done | bytes 2097168 | tf_op jit(solution)/shard_map/all_gather | solution.py:203
  386.0 18.0 %fusion.47 = f32[2,2,2048,512,2]{3,2,4,1,0:T(8,128)} fusion(bf16[2,2048,2,128]{3,1,2,0:T(8,128)(2,1)} %all-gather.23.cloned.1.call-done, bf16[2,512,2,2,64]{4,1,3,2,0:T(8,128)(2,1)} %bitcast.298, bf16[2,512,2,2,64]{4,1,3,2,0:T(8,128)(2,1)S(1)} %bitcast.295), kind=kOutput, calls=%fused_computation.86 | convolution fusion | flops 2149580800 | bytes 36700160 | tf_op jit(solution)/shard_map/bqkgd,btkd->bqkgt/dot_general | solution.py:208
  404.0 35.1 %all-reduce.19.cloned.1.call-done = bf16[2,512,1024]{2,1,0:T(8,128)(2,1)} async-done(((bf16[2,512,1024]{2,1,0:T(8,128)(2,1)}), bf16[2,512,1024]{2,1,0:T(8,128)(2,1)}) %all-reduce.19.cloned.1.call-update) | async-done | bytes 2097168 | tf_op jit(solution)/shard_map/psum | solution.py:191
  439.1 4.0 fusion.29
  443.2 5.6 multiply_reduce_fusion.2
  448.8 37.5 %all-gather.25.cloned.1.call-done = bf16[2,2048,2,128]{3,1,2,0:T(8,128)(2,1)} async-done(((bf16[2,512,2,128]{3,1,2,0:T(8,128)(2,1)}), bf16[2,2048,2,128]{3,1,2,0:T(8,128)(2,1)}) %all-gather.25.cloned.1.call-update) | async-done | bytes 2097168 | tf_op jit(solution)/shard_map/all_gather | solution.py:204
  486.3 24.6 %fusion.1 = bf16[2,512,2,2,2048]{1,4,3,2,0:T(8,128)(2,1)} fusion(f32[2,2,2048,512,2]{3,2,4,1,0:T(8,128)} %fusion.47, f32[2,512,2,2]{1,3,2,0:T(2,128)S(1)} %get-tuple-element.77, f32[2,512,2,2]{1,3,2,0:T(2,128)S(1)} %get-tuple-element.40, pred[2,512,2048]{1,2,0:T(8,128)(4,1)} %and_and_fusion, bf16[2,512,2,2,128]{1,4,3,2,0:T(8,128)(2,1)} %get-tuple-element.78, ...), kind=kOutput, calls=%fused_computation.2 | convolution fusion | flops 2214592512 | bytes 55607296 | tf_op jit(solution)/shard_map/bqkgd,btkd->bqkgt/dot_general | solution.py:222
  510.9 12.0 %fusion.38 = bf16[2,2048,2,128]{3,1,2,0:T(8,128)(2,1)} fusion(bf16[2,512,2,2,2048]{1,4,3,2,0:T(8,128)(2,1)} %fusion.1, bf16[2,512,2,2,64]{4,1,3,2,0:T(8,128)(2,1)} %bitcast.299, bf16[2,512,2,2,64]{4,1,3,2,0:T(8,128)(2,1)S(1)} %bitcast.296), kind=kOutput, calls=%fused_computation.76 | convolution fusion | flops 2151677952 | bytes 19922944 | tf_op jit(solution)/shard_map/bqkgt,bqkgd->btkd/dot_general | solution.py:231
  523.0 19.1 %fusion.39 = bf16[2,2048,2,128]{1,3,2,0:T(8,128)(2,1)} fusion(bf16[2,512,2,2,128]{1,4,3,2,0:T(8,128)(2,1)} %get-tuple-element.78, f32[2,2,2048,512,2]{3,2,4,1,0:T(8,128)} %fusion.47, f32[2,512,2,2]{1,3,2,0:T(2,128)S(1)} %get-tuple-element.40, pred[2,512,2048]{1,2,0:T(8,128)(4,1)} %and_and_fusion), kind=kOutput, calls=%fused_computation.77 | convolution fusion | flops 2198863872 | bytes 38813696 | tf_op jit(solution)/shard_map/bqkgt,bqkgd->btkd/dot_general | solution.py:216
  542.2 5.6 fusion.51
  549.1 9.0 fusion.62
  564.9 5.1 bitcast_convert_fusion.4
  570.0 5.1 bitcast_convert_fusion.3
  575.2 5.2 bitcast_convert_fusion.2
  591.9 5.0 convolution_convert_fusion
  596.9 14.2 %reduce-scatter.12.cloned.1.call-done = bf16[2,512,2,128]{1,3,2,0:T(8,128)(2,1)} async-done(((bf16[2,2048,2,128]{1,3,2,0:T(8,128)(2,1)}), bf16[2,512,2,128]{1,3,2,0:T(8,128)(2,1)}) %reduce-scatter.12.cloned.1.call-update) | async-done | bytes 524304 | tf_op jit(solution)/shard_map/reduce_scatter | solution.py:241
  620.2 12.8 %reduce-scatter.20.cloned.1.call-done = bf16[512,512]{1,0:T(8,128)(2,1)} async-done(((bf16[512,1024]{1,0:T(8,128)(2,1)}), bf16[512,512]{1,0:T(8,128)(2,1)}) %reduce-scatter.20.cloned.1.call-update) | async-done | bytes 524304 | tf_op jit(solution)/shard_map/reduce_scatter | solution.py:302
  633.0 22.5 %reduce-scatter.14.cloned.1.call-done = bf16[512,512]{1,0:T(8,128)(2,1)} async-done(((bf16[1024,512]{1,0:T(8,128)(2,1)}), bf16[512,512]{1,0:T(8,128)(2,1)}) %reduce-scatter.14.cloned.1.call-update) | async-done | bytes 524304 | tf_op jit(solution)/shard_map/reduce_scatter | solution.py:287
  655.5 28.8 %reduce-scatter.22.cloned.1.call-done = bf16[512,768]{1,0:T(8,128)(2,1)} async-done(((bf16[1024,768]{1,0:T(8,128)(2,1)}), bf16[512,768]{1,0:T(8,128)(2,1)}) %reduce-scatter.22.cloned.1.call-update) | async-done | bytes 786448 | tf_op jit(solution)/shard_map/reduce_scatter | solution.py:308
  684.4 28.9 %reduce-scatter.24.cloned.1.call-done = bf16[512,768]{1,0:T(8,128)(2,1)} async-done(((bf16[1024,768]{1,0:T(8,128)(2,1)}), bf16[512,768]{1,0:T(8,128)(2,1)}) %reduce-scatter.24.cloned.1.call-update) | async-done | bytes 786448 | tf_op jit(solution)/shard_map/reduce_scatter | solution.py:311
  713.2 28.3 %reduce-scatter.26.cloned.1.call-done = bf16[768,512]{1,0:T(8,128)(2,1)} async-done(((bf16[768,1024]{1,0:T(8,128)(2,1)}), bf16[768,512]{1,0:T(8,128)(2,1)}) %reduce-scatter.26.cloned.1.call-update) | async-done | bytes 786448 | tf_op jit(solution)/shard_map/reduce_scatter | solution.py:314
  741.5 17.3 %reduce-scatter.16.cloned.1.call-done = bf16[512,256]{1,0:T(8,128)(2,1)} async-done(((bf16[1024,256]{1,0:T(8,128)(2,1)}), bf16[512,256]{1,0:T(8,128)(2,1)}) %reduce-scatter.16.cloned.1.call-update) | async-done | bytes 262160 | tf_op jit(solution)/shard_map/reduce_scatter | solution.py:290
  758.8 17.5 %reduce-scatter.18.cloned.1.call-done = bf16[512,256]{1,0:T(8,128)(2,1)} async-done(((bf16[1024,256]{1,0:T(8,128)(2,1)}), bf16[512,256]{1,0:T(8,128)(2,1)}) %reduce-scatter.18.cloned.1.call-update) | async-done | bytes 262160 | tf_op jit(solution)/shard_map/reduce_scatter | solution.py:293
  777.7 87.1 %all-reduce.21.cloned.1.call-done = (bf16[2,512,1024]{2,1,0:T(8,128)(2,1)}, bf16[2,512,1024]{2,1,0:T(8,128)(2,1)}) async-done(((bf16[2,512,1024]{2,1,0:T(8,128)(2,1)}, bf16[2,512,1024]{2,1,0:T(8,128)(2,1)}), (bf16[2,512,1024]{2,1,0:T(8,128)(2,1)}, bf16[2,512,1024]{2,1,0:T(8,128)(2,1)})) %all-reduce.21.cloned.1.call-update) | async-done | bytes 4194320 | tf_op jit(solution)/shard_map/psum | solution.py:165
  864.7 3.4 fusion.33
  868.2 5.0 all-reduce.10
  873.5 6.0 all-reduce.6
  879.5 12.6 %all-reduce.8 = (bf16[512]{0:T(512)(128)(2,1)S(1)}, bf16[64]{0:T(256)(128)(2,1)S(1)}, bf16[64]{0:T(256)(128)(2,1)S(1)}, bf16[512]{0:T(512)(128)(2,1)S(1)}) all-reduce(bf16[512]{0:T(512)(128)(2,1)S(1)} %dynamic-slice.3, bf16[64]{0:T(256)(128)(2,1)S(1)} %get-tuple-element.17, ...), channel_id=1, replica_groups=mesh['fsdp'=2,'ctx'=4,'tp'=4] {'ctx'}, use_global_device_ids=true, to_apply=%region_21.22 | all-reduce | flops 1152 | bytes 4608 | tf_op jit(solution)/shard_map/psum | solution.py:319
  894.3 8.0 fusion.24
  902.4 112.5 %all-reduce.23.cloned.1.call-done = (bf16[512,512]{1,0:T(8,128)(2,1)}, bf16[512,256]{1,0:T(8,128)(2,1)}, bf16[512,256]{1,0:T(8,128)(2,1)}, bf16[512,512]{1,0:T(8...) async-done(((bf16[512,512]{1,0:T(8,128)(2,1)}, bf16[512,256]{1,0:T(8,128)(2,1)}, bf16[512,256]{1,0:T(8,128)(2,1)}, ...) | async-done | bytes 3932176 | tf_op jit(solution)/shard_map/psum | solution.py:320
  (259 shorter events, 92.9 us)
Async XLA Ops:
  7.2 10.4 %copy-start.36 = (bf16[512,256]{1,0:T(8,128)(2,1)S(1)}, bf16[512,256]{1,0:T(8,128)(2,1)}, u32[]{:S(2)}) copy-start(bf16[512,256]{1,0:T(8,128)(2,1)} %param.18) | copy-start | bytes 786436
  7.2 23.9 %copy-start.33 = (s32[2,2048]{1,0:T(2,128)S(1)}, s32[2,2048]{1,0:T(2,128)}, u32[]{:S(2)}) copy-start(s32[2,2048]{1,0:T(2,128)} %param.15) | copy-start | bytes 49156
  7.2 25.1 %copy-start.37 = (bf16[512,256]{1,0:T(8,128)(2,1)S(1)}, bf16[512,256]{1,0:T(8,128)(2,1)}, u32[]{:S(2)}) copy-start(bf16[512,256]{1,0:T(8,128)(2,1)} %param.19) | copy-start | bytes 786436
  7.2 35.3 %copy-start = (bf16[2,512,1024]{2,1,0:T(8,128)(2,1)S(1)}, bf16[2,512,1024]{2,1,0:T(8,128)(2,1)}, u32[]{:S(2)}) copy-start(bf16[2,512,1024]{2,1,0:T(8,128)(2,1)} %param.14) | copy-start | bytes 6291460
  7.2 64.9 %all-gather.13.cloned.1.call-start = ((), (), s32[]{:S(2)}) async-start(), calls=%async_computation.10 | async-start | bytes 1572864 | tf_op jit(solution)/shard_map/all_gather | solution.py:59
  9.5 139.1 %all-gather.11.cloned.1.call-start = ((), (), s32[]{:S(2)}) async-start(), calls=%async_computation.9 | async-start | bytes 5242880 | tf_op jit(solution)/shard_map/all_gather | solution.py:128
  15.5 56.6 %copy-start.42 = (f32[2,1,512]{2,1,0:T(1,128)}, f32[2,1,512]{2,1,0:T(1,128)S(1)}, u32[]{:S(2)}) copy-start(f32[2,1,512]{2,1,0:T(1,128)S(1)} %convert_element_type.277) | copy-start | bytes 12292
  17.6 54.5 %copy-start.44 = (f32[2,512]{1,0:T(2,128)}, f32[2,512]{1,0:T(2,128)S(1)}, u32[]{:S(2)}) copy-start(f32[2,512]{1,0:T(2,128)S(1)} %add_rsqrt_fusion.3) | copy-start | bytes 12292
  31.1 13.3 %copy-start.22 = (bf16[1024,256]{0,1:T(8,128)(2,1)}, bf16[1024,256]{0,1:T(8,128)(2,1)S(1)}, u32[]{:S(2)}) copy-start(bf16[1024,256]{0,1:T(8,128)(2,1)S(1)} %all_gather.50) | copy-start | bytes 1572868
  44.4 5.1 copy-start.50
  44.4 6.5 copy-start.54
  44.4 6.7 copy-start.55
  47.8 27.5 %copy-start.14 = (f32[2,512,64]{1,2,0:T(8,128)}, f32[2,512,64]{1,2,0:T(8,128)S(1)}, u32[]{:S(2)}) copy-start(f32[2,512,64]{1,2,0:T(8,128)S(1)} %get-tuple-element.66) | copy-start | bytes 786436
  49.5 14.4 %copy-start.5 = (f32[2,512,2,128]{3,1,2,0:T(8,128)}, f32[2,512,2,128]{3,1,2,0:T(8,128)S(1)}, u32[]{:S(2)}) copy-start(f32[2,512,2,128]{3,1,2,0:T(8,128)S(1)} %copy.230) | copy-start | bytes 3145732
  56.3 7.6 copy-start.48
  66.2 130.9 %all-gather.15.cloned.1.call-start = ((), (), s32[]{:S(2)}) async-start(), calls=%async_computation.11 | async-start | bytes 1572864 | tf_op jit(solution)/shard_map/all_gather | solution.py:64
  66.9 185.2 %all-reduce.17.cloned.1.call-start = ((), (), s32[]{:S(2)}) async-start(), calls=%async_computation.12 | async-start | bytes 4194304 | tf_op jit(solution)/shard_map/psum | solution.py:155
  67.0 7.8 copy-start.46
  78.9 85.9 %copy-start.16 = (bf16[2,512,4,64]{3,1,2,0:T(8,128)(2,1)}, bf16[2,512,4,64]{3,1,2,0:T(8,128)(2,1)S(1)}, u32[]{:S(2)}) copy-start(bf16[2,512,4,64]{3,1,2,0:T(8,128)(2,1)S(1)} %copy.236) | copy-start | bytes 1572868
  148.6 16.3 %copy-start.7 = (pred[2,512,2048]{1,2,0:T(8,128)(4,1)S(1)}, pred[2,512,2048]{1,2,0:T(8,128)(4,1)}, u32[]{:S(2)}) copy-start(pred[2,512,2048]{1,2,0:T(8,128)(4,1)} %and_and_fusion) | copy-start | bytes 6291460
  201.8 78.9 %all-gather.19.cloned.1.call-start = ((), (), s32[]{:S(2)}) async-start(), calls=%async_computation.14 | async-start | bytes 2359296 | tf_op jit(solution)/shard_map/all_gather | solution.py:67
  202.4 106.9 %all-gather.17.cloned.1.call-start = ((), (), s32[]{:S(2)}) async-start(), calls=%async_computation.13 | async-start | bytes 2359296 | tf_op jit(solution)/shard_map/all_gather | solution.py:66
  203.0 135.1 %all-gather.21.cloned.1.call-start = ((), (), s32[]{:S(2)}) async-start(), calls=%async_computation.15 | async-start | bytes 2359296 | tf_op jit(solution)/shard_map/all_gather | solution.py:68
  203.7 182.2 %all-gather.23.cloned.1.call-start = ((), (), s32[]{:S(2)}) async-start(), calls=%async_computation.17 | async-start | bytes 2621440 | tf_op jit(solution)/shard_map/all_gather | solution.py:203
  204.9 234.2 %all-reduce.19.cloned.1.call-start = ((), (), s32[]{:S(2)}) async-start(), calls=%async_computation.16 | async-start | bytes 4194304 | tf_op jit(solution)/shard_map/psum | solution.py:191
  338.1 8.0 copy-start.53
  351.9 34.1 %copy-start.17 = (bf16[2,512,4,64]{3,1,2,0:T(8,128)(2,1)S(1)}, bf16[2,512,4,64]{3,1,2,0:T(8,128)(2,1)}, u32[]{:S(2)}) copy-start(bf16[2,512,4,64]{3,1,2,0:T(8,128)(2,1)} %copy-done.16) | copy-start | bytes 1572868
  351.9 134.4 %all-gather.25.cloned.1.call-start = ((), (), s32[]{:S(2)}) async-start(), calls=%async_computation.18 | async-start | bytes 2621440 | tf_op jit(solution)/shard_map/all_gather | solution.py:204
  352.5 229.1 %reduce-scatter.10.cloned.1.call-start = ((), (), s32[]{:S(2)}) async-start(), calls=%async_computation.19 | async-start | bytes 2621440 | tf_op jit(solution)/shard_map/reduce_scatter | solution.py:238
  522.9 19.2 %copy-start.47 = (f32[128]{0:T(128)S(1)}, f32[128]{0:T(128)}, u32[]{:S(2)}) copy-start(f32[128]{0:T(128)} %copy-done.46) | copy-start | bytes 1540
  523.0 19.2 %copy-start.57 = (bf16[2,512,2,2,128]{1,4,3,2,0:T(8,128)(2,1)S(1)}, bf16[2,512,2,2,128]{1,4,3,2,0:T(8,128)(2,1)}, u32[]{:S(2)}) copy-start(bf16[2,512,2,2,128]{1,4,3,2,0:T(8,128)(2,1)} %copy-done.56) | copy-start | bytes 3145732
  523.0 88.1 %reduce-scatter.12.cloned.1.call-start = ((), (), s32[]{:S(2)}) async-start(), calls=%async_computation.20 | async-start | bytes 2621440 | tf_op jit(solution)/shard_map/reduce_scatter | solution.py:241
  542.1 90.9 %reduce-scatter.20.cloned.1.call-start = ((), (), s32[]{:S(2)}) async-start(), calls=%async_computation.24 | async-start | bytes 1572864 | tf_op jit(solution)/shard_map/reduce_scatter | solution.py:302
  548.9 9.2 copy-start.15
  548.9 9.2 copy-start.21
  548.9 106.6 %reduce-scatter.14.cloned.1.call-start = ((), (), s32[]{:S(2)}) async-start(), calls=%async_computation.21 | async-start | bytes 1572864 | tf_op jit(solution)/shard_map/reduce_scatter | solution.py:287
  564.8 119.5 %reduce-scatter.22.cloned.1.call-start = ((), (), s32[]{:S(2)}) async-start(), calls=%async_computation.25 | async-start | bytes 2359296 | tf_op jit(solution)/shard_map/reduce_scatter | solution.py:308
  570.0 143.3 %reduce-scatter.24.cloned.1.call-start = ((), (), s32[]{:S(2)}) async-start(), calls=%async_computation.26 | async-start | bytes 2359296 | tf_op jit(solution)/shard_map/reduce_scatter | solution.py:311
  575.1 166.4 %reduce-scatter.26.cloned.1.call-start = ((), (), s32[]{:S(2)}) async-start(), calls=%async_computation.27 | async-start | bytes 2359296 | tf_op jit(solution)/shard_map/reduce_scatter | solution.py:314
  575.2 6.5 copy-start.49
  580.3 178.5 %reduce-scatter.16.cloned.1.call-start = ((), (), s32[]{:S(2)}) async-start(), calls=%async_computation.22 | async-start | bytes 786432 | tf_op jit(solution)/shard_map/reduce_scatter | solution.py:290
  591.9 184.4 %reduce-scatter.18.cloned.1.call-start = ((), (), s32[]{:S(2)}) async-start(), calls=%async_computation.23 | async-start | bytes 786432 | tf_op jit(solution)/shard_map/reduce_scatter | solution.py:293
  614.0 250.7 %all-reduce.21.cloned.1.call-start = ((), (), s32[]{:S(2)}) async-start(), calls=%async_computation.28 | async-start | bytes 8388608 | tf_op jit(solution)/shard_map/psum | solution.py:165
  620.2 394.7 %all-reduce.23.cloned.1.call-start = ((), (), s32[]{:S(2)}) async-start(), calls=%async_computation.29 | async-start | bytes 7864320 | tf_op jit(solution)/shard_map/psum | solution.py:320
  1014.8 4.9 copy-start.29
  1014.8 6.3 copy-start.32
  1017.3 4.9 copy-start.31
  1019.8 4.4 copy-start.34
  (33 other events, 69.8 us)
Sparse Core Ops, SparseCore 0:
  10.1 30.1 all-gather.12
  66.3 82.2 all-gather.10
  150.1 19.7 all-gather.14
  201.9 50.0 all-reduce.16
  253.5 27.2 all-gather.18
  282.1 27.1 all-gather.16
  310.9 27.1 all-gather.20
  340.3 45.6 all-gather.22
  388.9 50.1 all-reduce.18
  440.5 45.7 all-gather.24
  523.1 42.4 reduce-scatter.9
  568.2 42.8 reduce-scatter.11
  613.3 19.5 reduce-scatter.19
  635.1 20.3 reduce-scatter.13
  658.2 26.1 reduce-scatter.21
  687.0 26.1 reduce-scatter.23
  715.3 26.1 reduce-scatter.25
  744.2 14.6 reduce-scatter.15
  761.6 14.6 reduce-scatter.17
  779.2 85.5 all-reduce.20
  867.7 147.0 all-reduce.22
